TPU v7x, 256 devices: a whole 4x4x8 slice. The times are simulated.
256 devices in a mesh: chan: 4 (over z_hi), pulse: 32 (over x, y, core), range: 2 (over z_lo).
Axes of the slice: x: 4, y: 4, z: 8 (z_hi: 4, z_lo: 2; z = z_hi * 2 + z_lo), core: 2. Of those that a mesh axis runs over, the one named last changes fastest.
Arguments:
- signal: bfloat16 [2, 64, 256, 8192], P(None, 'chan', 'pulse', 'range'), may hold values from -6 to 6
- steering: bfloat16 [2, 32, 64], replicated, may hold values from -0.5 to 0.5
- spectrum: float32 [2, 8192], replicated, may hold values from -6 to 6
Outputs:
- detection: float32 [32, 256, 8192], P('chan', 'pulse', 'range')
All inputs are finite; a program needn't handle non-finite values.
Results may differ from a plain program's by a relative error of at most 0.0087.
Values may be sent and summed in bfloat16 or wider, within the bound.
A program may use at most 64 MiB of HBM per device.

v0:
```python
import math

import jax
import jax.numpy as jnp
import numpy as np
from jax import lax
from jax.experimental import pallas as pl
from jax.experimental.pallas import tpu as pltpu
from jax.sharding import PartitionSpec as P

F32, BF16 = jnp.float32, jnp.bfloat16
MESH = pl.DeviceIdType.MESH
GUARD, TRAIN, NOISE_FLOOR = 4, 16, 0.25
NZ, NQ = 8, 32
HOPS = (4, 3, -3, 2, -2, 1, -1)
GROUPS = (2, 1, 3, 0)


def times(v, angle_num, period, sign):
    k = angle_num % period
    if k == 0:
        return v
    re, im = v
    if 4 * k == period:
        return (-im, re) if sign > 0 else (im, -re)
    if 2 * k == period:
        return (-re, -im)
    if 4 * k == 3 * period:
        return (im, -re) if sign > 0 else (-im, re)
    c = math.cos(2 * math.pi * k / period)
    s = sign * math.sin(2 * math.pi * k / period)
    return (re * c - im * s, re * s + im * c)


def dft(xs, sign):
    n = len(xs)
    if n == 1:
        return xs
    even, odd = dft(xs[0::2], sign), dft(xs[1::2], sign)
    odd = [times(v, k, n, sign) for k, v in enumerate(odd)]
    plus = [(a[0] + b[0], a[1] + b[1]) for a, b in zip(even, odd)]
    minus = [(a[0] - b[0], a[1] - b[1]) for a, b in zip(even, odd)]
    return plus + minus


def pair(x):
    x = x.astype(F32)
    return (x[:8], x[8:])


def joined(v):
    return jnp.concatenate(v, axis=0)


def lane_tables():
    n = np.arange(128)
    ang = 2 * np.pi * (np.outer(n, n) % 128) / 128
    c, s = np.cos(ang), np.sin(ang)
    ahead = np.block([[c, -s], [s, c]])
    back = np.block([[c, s], [-s, c]])
    k1 = (np.arange(8)[:, None] + 8 * np.arange(8)[None, :]).reshape(-1)
    turn = 2 * np.pi * np.outer(k1, n) / 8192
    twist = np.stack([np.cos(turn), -np.sin(turn)])
    return np.stack([ahead, back]), twist


def band_table():
    gap = np.abs(np.arange(512)[:, None] - (128 + np.arange(256)[None, :]))
    return ((gap > GUARD) & (gap <= GUARD + TRAIN)).astype(np.float32)


def spread(rows):
    return jnp.broadcast_to(rows[:, None, :], (8, 8, 128)).reshape(64, 128)


def zdev(z):
    return {"chan": z // 2, "range": lax.rem(z, 2)}


def kernel(
    sig, w, resp, lanes, twist, band, out,
    wide, send, recv, beams, mid, mid2, lhs, prod, comp, crossed, cols, dmid, power, rows, halo, win, noise, turned,
    ss1, rs1, ss2, rs2, ss3, rs3, ss4, rs4, ss5, rs5,
):
    c, q, r = lax.axis_index("chan"), lax.axis_index("pulse"), lax.axis_index("range")
    me = c * 2 + r
    bar = pltpu.get_barrier_semaphore()
    for d in range(1, NZ):
        pl.semaphore_signal(bar, inc=1, device_id=zdev(lax.rem(me + d, NZ)), device_id_type=MESH)

    def greet(d, carry):
        pl.semaphore_signal(bar, inc=1, device_id={"pulse": lax.rem(q + d, NQ)}, device_id_type=MESH)
        return carry

    lax.fori_loop(1, NQ, greet, 0)

    def widen(t, carry):
        x = sig[:, :, :, pl.ds(pl.multiple_of(t * 128, 128), 128)].astype(F32)
        wide[t] = x.reshape(256, 128)
        return carry

    lax.fori_loop(0, 32, widen, 0)

    def hop(k):
        t = lax.rem(me + HOPS[k] + NZ, NZ)
        return t, pltpu.make_async_remote_copy(
            src_ref=send.at[t], dst_ref=recv.at[me], send_sem=ss1.at[k], recv_sem=rs1.at[k],
            device_id=zdev(t), device_id_type=MESH,
        )

    def take_pulse(j):
        def one(t, carry):
            send[j, t] = wide[t, pl.ds(j, 32, stride=8), :].astype(BF16)
            return carry

        lax.fori_loop(0, 32, one, 0, unroll=4)

    for k in range(7):
        t, copy = hop(k)
        take_pulse(t)
        if k == 0:
            pl.semaphore_wait(bar, NZ - 1 + NQ - 1)
        copy.start()

    def own(t, carry):
        recv[me, t] = wide[t, pl.ds(me, 32, stride=8), :].astype(BF16)
        return carry

    lax.fori_loop(0, 32, own, 0, unroll=4)
    for k in range(7):
        hop(k)[1].wait()

    for half in range(2):

        def form(i, carry, half=half):
            cols2 = [jnp.concatenate([recv[2 * cc + half, 2 * i + e] for cc in range(4)], axis=0) for e in range(2)]
            got = jnp.dot(w[...], jnp.concatenate(cols2, axis=1), preferred_element_type=F32).astype(BF16)
            for e in range(2):
                beams[half * 32 + 2 * i + e] = got[:, e * 128 : (e + 1) * 128].reshape(4, 16, 128)
            return carry

        lax.fori_loop(0, 16, form, 0)

    def cross(g, d):
        t = lax.rem(q + d, NQ)
        return pltpu.make_async_remote_copy(
            src_ref=comp.at[g, :, t], dst_ref=crossed.at[g, :, q], send_sem=ss2.at[g], recv_sem=rs2.at[g],
            device_id={"pulse": t}, device_id_type=MESH,
        )

    def filter_group(g):
        for b in range(8):
            ys = dft([pair(beams[8 * a + b, g]) for a in range(8)], -1)
            for ka in range(8):
                mid[b * 8 + ka] = joined(times(ys[ka], b * ka, 64, -1))
        for ka in range(8):
            xs = dft([pair(mid[b * 8 + ka]) for b in range(8)], -1)
            tr, ti = twist[0, ka * 8 : ka * 8 + 8, :], twist[1, ka * 8 : ka * 8 + 8, :]
            tr, ti = spread(tr), spread(ti)
            re = jnp.concatenate([v[0] for v in xs], axis=0)
            im = jnp.concatenate([v[1] for v in xs], axis=0)
            lhs[ka * 64 : ka * 64 + 64, 0:128] = (re * tr - im * ti).astype(BF16)
            lhs[ka * 64 : ka * 64 + 64, 128:256] = (re * ti + im * tr).astype(BF16)
        prod[...] = jnp.dot(lhs[...], lanes[0], preferred_element_type=F32)
        for ka in range(8):
            hr, hi = spread(resp[0, ka * 8 : ka * 8 + 8, :]), spread(resp[1, ka * 8 : ka * 8 + 8, :])
            re, im = prod[ka * 64 : ka * 64 + 64, 0:128], prod[ka * 64 : ka * 64 + 64, 128:256]
            lhs[ka * 64 : ka * 64 + 64, 0:128] = (re * hr - im * hi).astype(BF16)
            lhs[ka * 64 : ka * 64 + 64, 128:256] = (re * hi + im * hr).astype(BF16)
        prod[...] = jnp.dot(lhs[...], lanes[1], preferred_element_type=F32)
        for ka in range(8):
            tr, ti = spread(twist[0, ka * 8 : ka * 8 + 8, :]), spread(twist[1, ka * 8 : ka * 8 + 8, :])
            re, im = prod[ka * 64 : ka * 64 + 64, 0:128], prod[ka * 64 : ka * 64 + 64, 128:256]
            re, im = re * tr + im * ti, im * tr - re * ti
            ys = dft([(re[8 * kb : 8 * kb + 8], im[8 * kb : 8 * kb + 8]) for kb in range(8)], 1)
            for b in range(8):
                mid2[b * 8 + ka] = joined(times(ys[b], b * ka, 64, 1))
        for b in range(8):
            xs = dft([pair(mid2[b * 8 + ka]) for ka in range(8)], 1)
            for a in range(8):
                n1 = 8 * a + b
                comp[g, n1 // 32, n1 % 32] = joined(xs[a]).astype(BF16)

    def group(step):
        offset = jnp.where(step == 0, 2, jnp.where(step == 1, 1, jnp.where(step == 2, 3, 0)))
        return lax.rem(c + offset, 4)

    def each_group(step, carry):
        g = group(step)
        filter_group(g)

        def start(d, cc):
            cross(g, d).start()
            return cc

        lax.fori_loop(1, NQ, start, 0)
        for rr in range(2):
            crossed[g, rr, q] = comp[g, rr, q]
        return carry

    lax.fori_loop(0, 4, each_group, 0)

    def to_owner(k, g, rr):
        return pltpu.make_async_remote_copy(
            src_ref=crossed.at[g, rr], dst_ref=cols.at[me], send_sem=ss3.at[k], recv_sem=rs3.at[k],
            device_id={"chan": g, "range": rr}, device_id_type=MESH,
        )

    moves = []
    for step, offset in enumerate(GROUPS):
        g = lax.rem(c + offset, 4)
        for e in range(2):
            if offset == 0 and e == 0:
                continue
            moves.append((len(moves), step, g, lax.rem(r + e, 2)))
    seen = -1
    for k, step, g, rr in moves:
        if step != seen:
            whole = crossed.at[g, :, pl.ds(0, NQ - 1)]
            pltpu.make_async_copy(whole, whole, rs2.at[g]).wait()
            seen = step
        to_owner(k, g, rr).start()

    def keep(t, carry):
        cols[me, t] = crossed[c, r, t]
        return carry

    lax.fori_loop(0, NQ, keep, 0, unroll=4)
    for k, step, g, rr in moves:
        to_owner(k, g, rr).wait()
    for g in range(4):
        whole = comp.at[g, :, pl.ds(0, NQ - 1)]
        pltpu.make_async_copy(whole, whole, ss2.at[g]).wait()

    for b in range(16):
        ps = [16 * a + b for a in range(16)]
        ys = dft([pair(cols[p % 8, p // 8]) for p in ps], -1)
        for fa in range(16):
            dmid[b * 16 + fa] = joined(times(ys[fa], b * fa, 256, -1))
    for fa in range(16):
        xs = dft([pair(dmid[b * 16 + fa]) for b in range(16)], -1)
        for fb in range(16):
            re, im = xs[fb]
            power[fa + 16 * fb] = ((re * re + im * im) * (1.0 / 256)).astype(BF16)

    def to_bins(d):
        t = lax.rem(q + d, NQ)
        return pltpu.make_async_remote_copy(
            src_ref=power.at[pl.ds(t * 8, 8)], dst_ref=rows.at[q], send_sem=ss4.at[d], recv_sem=rs4.at[d],
            device_id={"pulse": t}, device_id_type=MESH,
        )

    def start_bins(d, carry):
        to_bins(d).start()
        return carry

    def wait_bins(d, carry):
        to_bins(d).wait()
        return carry

    lax.fori_loop(1, NQ, start_bins, 0)
    for f in range(8):
        rows[q, f] = power[q * 8 + f]
    lax.fori_loop(1, NQ, wait_bins, 0)
    edge = pltpu.make_async_remote_copy(
        src_ref=rows.at[(1 - r) * (NQ - 1)], dst_ref=halo, send_sem=ss5, recv_sem=rs5,
        device_id={"range": 1 - r}, device_id_type=MESH,
    )
    edge.start()

    def flat(x):
        return x.astype(F32).reshape(64, 128).astype(BF16)

    def place(i, tile, x):
        win[i, :, tile * 128 : (tile + 1) * 128] = x

    for i in range(16):
        x0, x1 = flat(rows[2 * i]), flat(rows[2 * i + 1])
        place(i, 1, x0)
        place(i, 2, x1)
        if i > 0:
            place(i - 1, 3, x0)
        if i < 15:
            place(i + 1, 0, x1)
    edge.wait()
    beside = halo[...].astype(F32).reshape(64, 128)
    right = r.astype(F32)
    place(0, 0, (beside * right).astype(BF16))
    place(15, 3, (beside * (1.0 - right)).astype(BF16))
    noise[...] = jnp.dot(win[...].reshape(1024, 512), band[...], preferred_element_type=F32)
    for i in range(16):
        for e in range(2):
            level = noise[i * 64 : (i + 1) * 64, e * 128 : (e + 1) * 128] * (1.0 / (2 * TRAIN)) + NOISE_FLOOR
            got = rows[2 * i + e].astype(F32).reshape(64, 128) / level
            at = (2 * i + e) * 128
            for f in range(8):
                turned[2 * i + e, pl.ds(f, 8, stride=8), :] = got[f * 8 : f * 8 + 8]
            out[:, at : at + 128] = turned[2 * i + e]


def shards(signal, steering, spectrum):
    lanes, twist = lane_tables()
    wr, wi = (x.reshape(4, 8, 4, 16).transpose(0, 1, 2, 3) for x in (steering[0], steering[1]))
    top = jnp.stack([wr, -wi], axis=3)
    low = jnp.stack([wi, wr], axis=3)
    w = jnp.stack([top, low], axis=1).reshape(64, 128)
    resp = spectrum.reshape(2, 128, 8, 8).transpose(0, 3, 2, 1).reshape(2, 64, 128) * (1.0 / 8192)
    vm = pl.BlockSpec(memory_space=pltpu.VMEM)
    scratch = [
        pltpu.VMEM((32, 256, 128), F32),
        pltpu.VMEM((8, 32, 32, 128), BF16),
        pltpu.VMEM((8, 32, 32, 128), BF16),
        pltpu.VMEM((64, 4, 16, 128), BF16),
        pltpu.VMEM((64, 16, 128), F32),
        pltpu.VMEM((64, 16, 128), F32),
        pltpu.VMEM((512, 256), BF16),
        pltpu.VMEM((512, 256), F32),
        pltpu.VMEM((4, 2, 32, 16, 128), BF16),
        pltpu.VMEM((4, 2, 32, 16, 128), BF16),
        pltpu.VMEM((8, 32, 16, 128), BF16),
        pltpu.VMEM((256, 16, 128), F32),
        pltpu.VMEM((256, 8, 128), BF16),
        pltpu.VMEM((32, 8, 8, 128), BF16),
        pltpu.VMEM((8, 8, 128), BF16),
        pltpu.VMEM((16, 64, 512), BF16),
        pltpu.VMEM((1024, 256), F32),
        pltpu.VMEM((32, 64, 128), F32),
        pltpu.SemaphoreType.DMA((7,)), pltpu.SemaphoreType.DMA((7,)),
        pltpu.SemaphoreType.DMA((4,)), pltpu.SemaphoreType.DMA((4,)),
        pltpu.SemaphoreType.DMA((7,)), pltpu.SemaphoreType.DMA((7,)),
        pltpu.SemaphoreType.DMA((32,)), pltpu.SemaphoreType.DMA((32,)),
        pltpu.SemaphoreType.DMA, pltpu.SemaphoreType.DMA,
    ]
    got = pl.pallas_call(
        kernel,
        out_shape=jax.ShapeDtypeStruct((64, 4096), F32),
        in_specs=[vm] * 6,
        out_specs=vm,
        scratch_shapes=scratch,
        compiler_params=pltpu.CompilerParams(collective_id=0, has_side_effects=True, vmem_limit_bytes=60 * 2**20),
        name="radar",
    )(
        signal, w, resp, jnp.asarray(lanes, BF16), jnp.asarray(twist, F32), jnp.asarray(band_table(), BF16),
    )
    return got.reshape(8, 8, 4096)


def solution(mesh):
    return jax.shard_map(
        shards,
        mesh=mesh,
        in_specs=(P(None, "chan", "pulse", "range"), P(), P()),
        out_specs=P("chan", "pulse", "range"),
        check_vma=False,
    )
```

profile of v0, /device:TPU:1, one launch (start us, length us, event | category | flops | bytes accessed | tf_op | source)
XLA Modules:
  0.0 118.1 jit_solution(11405662819407848378)
XLA Ops:
  0.0 0.7 fusion
  0.7 0.1 reshape_squeeze.4
  0.8 0.1 neg.10
  0.9 0.1 stack_reshape_squeeze.6
  1.0 0.4 maximum_bitcast_fusion
  1.3 0.2 pad_maximum_fusion
  1.6 0.7 reshape.22.w
  2.3 0.9 broadcast_multiply_fusion
  3.2 0.6 mul.14
  3.8 1.0 copy.16
  4.7 111.1 %radar.1 = f32[64,4096]{1,0:T(8,128)} custom-call(bf16[2,16,8,4096]{3,2,1,0:T(8,128)(2,1)} %sig.1, bf16[64,128]{1,0:T(8,128)(2,1)} %reshape.22.w, f32[2,64,128]{2,1,0:T(8,128)} %bitcast.9, bf16[2,256,256]{2,1,0:T(8,128)(2,1)} %constant.8.clone.lanes, f32[2,64,128]{2,1,0:T(8,128)} %constant.9.clone.twist, bf16[512,256]{1,0:T(8,128)(2,1)} %constant.10.clone.band), custom_call_target="tpu_custom_call" | custom-call | tf_op jit(solution)/shard_map/radar/pallas_call | solution.py:334
  115.9 2.3 %copy.18 = f32[8,8,4096]{2,1,0:T(8,128)} copy(f32[8,8,4096]{2,1,0:T(8,128)} %bitcast.8) | data formatting | bytes 2097152
where the time goes:
time: 118 us
  Pallas kernels  111 us (94%)
  local copies, waits for them, and re-layouts  5.45 us (5%)
  other arithmetic  1.5 us (1%)
    pallas_call x1, Pallas kernels, shards(): pl.pallas_call(kernel, out_shape=jax.ShapeDtypeStruct((64, 4096), F32), i...  111 us

commit v1 on v0

v1 whole, which is shorter than its diff:
```python
import math

import jax
import jax.numpy as jnp
import numpy as np
from jax import lax
from jax.experimental import pallas as pl
from jax.experimental.pallas import tpu as pltpu
from jax.sharding import PartitionSpec as P

F32, BF16 = jnp.float32, jnp.bfloat16
MESH = pl.DeviceIdType.MESH
GUARD, TRAIN, NOISE_FLOOR = 4, 16, 0.25
NZ, NQ = 8, 32
HOPS = (4, 3, -3, 2, -2, 1, -1)
CHUNKS = 4
PEERS = sorted(
    ((x, y, k) for x in range(4) for y in range(4) for k in range(2) if x + y + k),
    key=lambda d: -(min(d[0], 4 - d[0]) + min(d[1], 4 - d[1])),
)


def times(v, angle_num, period, sign):
    k = angle_num % period
    if k == 0:
        return v
    re, im = v
    if 4 * k == period:
        return (-im, re) if sign > 0 else (im, -re)
    if 2 * k == period:
        return (-re, -im)
    if 4 * k == 3 * period:
        return (im, -re) if sign > 0 else (-im, re)
    c = math.cos(2 * math.pi * k / period)
    s = sign * math.sin(2 * math.pi * k / period)
    return (re * c - im * s, re * s + im * c)


def dft(xs, sign):
    n = len(xs)
    if n == 1:
        return xs
    even, odd = dft(xs[0::2], sign), dft(xs[1::2], sign)
    odd = [times(v, k, n, sign) for k, v in enumerate(odd)]
    plus = [(a[0] + b[0], a[1] + b[1]) for a, b in zip(even, odd)]
    minus = [(a[0] - b[0], a[1] - b[1]) for a, b in zip(even, odd)]
    return plus + minus


def pair(x):
    x = x.astype(F32)
    return (x[:8], x[8:])


def joined(v):
    return jnp.concatenate(v, axis=0)


def lane_tables():
    n = np.arange(128)
    k2 = 2 * (n % 64) + n // 64
    ang = 2 * np.pi * (np.outer(n, k2) % 128) / 128
    c, s = np.cos(ang), np.sin(ang)
    ahead = np.block([[c, -s], [s, c]])
    back = np.block([[c.T, s.T], [-s.T, c.T]])
    k1 = (np.arange(8)[:, None] + 8 * np.arange(8)[None, :]).reshape(-1)
    turn = 2 * np.pi * np.outer(k1, n) / 8192
    twist = np.stack([np.cos(turn), -np.sin(turn)])
    return np.stack([ahead, back]), twist


def spread(rows):
    return jnp.broadcast_to(rows[:, None, :], (8, 8, 128)).reshape(64, 128)


def zdev(z):
    return {"chan": z // 2, "range": lax.rem(z, 2)}


def qpeer(q, d):
    x, y, k = q // 8, lax.rem(q // 2, 4), lax.rem(q, 2)
    return lax.rem(x + d[0], 4) * 8 + lax.rem(y + d[1], 4) * 2 + lax.rem(k + d[2], 2)


def kernel(
    sig_hbm, steer_hbm, spec_hbm, lanes_hbm, twist_hbm, out,
    sig, steer, spec, lanes, twist, wmat, rowed, turned_resp, resp, tw, band,
    wide, send, recv, formed, mid, mid2, lhs, prod, comp, crossed, early, cols, dmid, power, rows, halo, win, noise, turned,
    loads, ss1, rs1, ss2, rs2, ss3, rs3, ss4, rs4, ss5, rs5, ss6, rs6,
):
    c, q, r = lax.axis_index("chan"), lax.axis_index("pulse"), lax.axis_index("range")
    me = c * 2 + r
    bar = pltpu.get_barrier_semaphore()
    for d in range(1, NZ):
        pl.semaphore_signal(bar, inc=1, device_id=zdev(lax.rem(me + d, NZ)), device_id_type=MESH)

    def greet(d, carry):
        pl.semaphore_signal(bar, inc=1, device_id={"pulse": lax.rem(q + d, NQ)}, device_id_type=MESH)
        return carry

    lax.fori_loop(1, NQ, greet, 0)
    fetched = [
        pltpu.make_async_copy(a, b, loads.at[i])
        for i, (a, b) in enumerate(
            [(sig_hbm, sig), (steer_hbm, steer), (spec_hbm, spec), (lanes_hbm, lanes), (twist_hbm, twist)]
        )
    ]
    for copy in fetched:
        copy.start()
    fetched[0].wait()

    def widen(t, carry):
        x = sig[:, :, :, pl.ds(pl.multiple_of(t * 128, 128), 128)].astype(F32)
        wide[t] = x.reshape(256, 128)
        return carry

    lax.fori_loop(0, 32, widen, 0, unroll=2)
    per = 8 // CHUNKS

    def take_pulse(j, part, into, at):
        for b in range(part * per, (part + 1) * per):
            for a in range(4):
                into[at, b, a] = wide[8 * a + b, pl.ds(j, 32, stride=8), :].astype(BF16)

    def hop(k, part):
        t = lax.rem(me + HOPS[k] + NZ, NZ)
        mine = pl.ds(part * per, per)
        return t, pltpu.make_async_remote_copy(
            src_ref=send.at[t, mine], dst_ref=recv.at[me, mine], send_sem=ss1.at[k, part], recv_sem=rs1.at[k, part],
            device_id=zdev(t), device_id_type=MESH,
        )

    for part in range(CHUNKS):
        for k in range(7):
            t, copy = hop(k, part)
            take_pulse(t, part, send, t)
            if k == 0 and part == 0:
                pl.semaphore_wait(bar, NZ - 1 + NQ - 1)
            copy.start()
    for part in range(CHUNKS):
        take_pulse(me, part, recv, me)

    for copy in fetched[1:]:
        copy.wait()
    wr, wi = steer[0].astype(F32), steer[1].astype(F32)
    wmat[0:32] = jnp.concatenate([wr, -wi], axis=1).astype(BF16)
    wmat[32:64] = jnp.concatenate([wi, wr], axis=1).astype(BF16)
    for i in range(2):
        for m in range(64):
            rowed[m : m + 1] = spec[i : i + 1, m * 128 : (m + 1) * 128]
        a = rowed[...] * (1.0 / 8192)
        both = jnp.concatenate([a, jnp.concatenate([a[:, 64:], a[:, :64]], axis=1)], axis=0)
        turned_resp[...] = jnp.transpose(both)
        for ka in range(8):
            resp[i, ka * 64 : ka * 64 + 64] = spread(turned_resp[pl.ds(ka, 8, stride=8), :])
            tw[i, ka * 64 : ka * 64 + 64] = spread(twist[i, ka * 8 : ka * 8 + 8])

    def make_band(i, carry):
        row = lax.broadcasted_iota(jnp.int32, (64, 256), 0) + i * 64
        gap = jnp.abs(row - 128 - lax.broadcasted_iota(jnp.int32, (64, 256), 1))
        ones = jnp.where((gap > GUARD) & (gap <= GUARD + TRAIN), 1.0, 0.0)
        band[pl.ds(pl.multiple_of(i * 64, 64), 64), :] = ones.astype(BF16)
        return carry

    lax.fori_loop(0, 8, make_band, 0)
    win[0, :, 0:128] = jnp.zeros((64, 128), BF16)
    win[15, :, 384:512] = jnp.zeros((64, 128), BF16)

    def front(b):
        now = b % 2
        for half in range(2):
            for a in (0, 2):
                blocks = []
                for e in range(2):
                    tiles = [recv[2 * cc + half, b, a + e] for cc in range(4)]
                    blocks.append(jnp.concatenate([t[:16] for t in tiles] + [t[16:] for t in tiles], axis=0))
                got = jnp.dot(wmat[...], jnp.concatenate(blocks, axis=1), preferred_element_type=F32)
                got = got.astype(BF16).astype(F32)
                for e in range(2):
                    formed[now, half * 4 + a + e] = got[:, e * 128 : (e + 1) * 128]
        for g in range(4):
            xs = [(formed[now, a, 8 * g : 8 * g + 8], formed[now, a, 32 + 8 * g : 40 + 8 * g]) for a in range(8)]
            ys = dft(xs, -1)
            for ka in range(8):
                mid[g, b * 8 + ka] = joined(times(ys[ka], b * ka, 64, -1))

    for part in range(CHUNKS):
        for k in range(7):
            hop(k, part)[1].wait_recv()
        for b in range(part * per, (part + 1) * per):
            front(b)

    def filter_group(g):
        for ka in range(8):
            here = slice(ka * 64, ka * 64 + 64)
            xs = dft([pair(mid[g, b * 8 + ka]) for b in range(8)], -1)
            tr, ti = tw[0, here], tw[1, here]
            re = jnp.concatenate([v[0] for v in xs], axis=0)
            im = jnp.concatenate([v[1] for v in xs], axis=0)
            lhs[here, 0:128] = (re * tr - im * ti).astype(BF16)
            lhs[here, 128:256] = (re * ti + im * tr).astype(BF16)
        prod[...] = jnp.dot(lhs[...], lanes[0], preferred_element_type=F32)
        for ka in range(8):
            here = slice(ka * 64, ka * 64 + 64)
            hr, hi = resp[0, here], resp[1, here]
            re, im = prod[here, 0:128], prod[here, 128:256]
            lhs[here, 0:128] = (re * hr - im * hi).astype(BF16)
            lhs[here, 128:256] = (re * hi + im * hr).astype(BF16)
        prod[...] = jnp.dot(lhs[...], lanes[1], preferred_element_type=F32)
        for ka in range(8):
            here = slice(ka * 64, ka * 64 + 64)
            tr, ti = tw[0, here], tw[1, here]
            re, im = prod[here, 0:128], prod[here, 128:256]
            re, im = re * tr + im * ti, im * tr - re * ti
            ys = dft([(re[8 * kb : 8 * kb + 8], im[8 * kb : 8 * kb + 8]) for kb in range(8)], 1)
            for b in range(8):
                mid2[b * 8 + ka] = joined(times(ys[b], b * ka, 64, 1))
        for b in range(8):
            xs = dft([pair(mid2[b * 8 + ka]) for ka in range(8)], 1)
            for a in range(8):
                n1 = 8 * a + b
                comp[g, n1 // 32, n1 % 32] = joined(xs[a]).astype(BF16)

    far = lax.rem(c + 2, 4)

    def far_copy(e):
        rr = lax.rem(r + e, 2)
        return pltpu.make_async_remote_copy(
            src_ref=comp.at[far, rr], dst_ref=early.at[r], send_sem=ss3.at[e], recv_sem=rs3.at[e],
            device_id={"chan": far, "range": rr}, device_id_type=MESH,
        )

    filter_group(far)
    for e in range(2):
        far_copy(e).start()

    def cross(g, d):
        t = qpeer(q, d)
        return pltpu.make_async_remote_copy(
            src_ref=comp.at[g, :, t], dst_ref=crossed.at[g, :, q], send_sem=ss2.at[g], recv_sem=rs2.at[g],
            device_id={"pulse": t}, device_id_type=MESH,
        )

    def each_group(step, carry):
        g = lax.rem(c + jnp.where(step == 0, 1, jnp.where(step == 1, 3, 0)), 4)
        filter_group(g)
        for d in PEERS:
            cross(g, d).start()
        for rr in range(2):
            crossed[g, rr, q] = comp[g, rr, q]
        return carry

    lax.fori_loop(0, 3, each_group, 0)

    def to_owner(k, g, rr):
        return pltpu.make_async_remote_copy(
            src_ref=crossed.at[g, rr], dst_ref=cols.at[me], send_sem=ss3.at[k], recv_sem=rs3.at[k],
            device_id={"chan": g, "range": rr}, device_id_type=MESH,
        )

    moves = []
    for offset in (1, 3, 0):
        g = lax.rem(c + offset, 4)
        whole = crossed.at[g, :, pl.ds(0, NQ - 1)]
        pltpu.make_async_copy(whole, whole, rs2.at[g]).wait()
        for e in range(2):
            if offset or e:
                moves.append(to_owner(2 + len(moves), g, lax.rem(r + e, 2)))
                moves[-1].start()

    def forward(d):
        t = qpeer(q, d)
        return pltpu.make_async_remote_copy(
            src_ref=early.at[:, t], dst_ref=cols.at[pl.ds(2 * far, 2), q], send_sem=ss6, recv_sem=rs6,
            device_id={"pulse": t}, device_id_type=MESH,
        )

    for e in range(2):
        far_copy(e).wait()
    for d in PEERS:
        forward(d).start()
    for rr in range(2):
        cols[2 * far + rr, q] = early[rr, q]

    def keep(t, carry):
        cols[me, t] = crossed[c, r, t]
        return carry

    lax.fori_loop(0, NQ, keep, 0, unroll=4)
    for part in range(CHUNKS):
        for k in range(7):
            hop(k, part)[1].wait_send()
    for move in moves:
        move.wait()
    whole = early.at[:, pl.ds(0, NQ - 1)]
    pltpu.make_async_copy(whole, whole, rs6).wait()
    pltpu.make_async_copy(whole, whole, ss6).wait()
    for offset in (1, 3, 0):
        g = lax.rem(c + offset, 4)
        whole = comp.at[g, :, pl.ds(0, NQ - 1)]
        pltpu.make_async_copy(whole, whole, ss2.at[g]).wait()

    for b in range(16):
        ps = [16 * a + b for a in range(16)]
        ys = dft([pair(cols[p % 8, p // 8]) for p in ps], -1)
        for fa in range(16):
            dmid[b * 16 + fa] = joined(times(ys[fa], b * fa, 256, -1))
    for fa in range(16):
        xs = dft([pair(dmid[b * 16 + fa]) for b in range(16)], -1)
        for fb in range(16):
            re, im = xs[fb]
            power[fa + 16 * fb] = ((re * re + im * im) * (1.0 / 256)).astype(BF16)

    def to_bins(i):
        t = qpeer(q, PEERS[i])
        return pltpu.make_async_remote_copy(
            src_ref=power.at[pl.ds(t * 8, 8)], dst_ref=rows.at[q], send_sem=ss4.at[i], recv_sem=rs4.at[q],
            device_id={"pulse": t}, device_id_type=MESH,
        )

    def from_bins(s):
        return pltpu.make_async_remote_copy(
            src_ref=power.at[pl.ds(s * 8, 8)], dst_ref=rows.at[s], send_sem=ss4.at[0], recv_sem=rs4.at[s],
            device_id={"pulse": s}, device_id_type=MESH,
        )

    for i in range(NQ - 1):
        to_bins(i).start()
    rows[q] = power[pl.ds(q * 8, 8)]
    outer = (1 - r) * (NQ - 1)

    @pl.when(q != outer)
    def _():
        from_bins(outer).wait_recv()

    edge = pltpu.make_async_remote_copy(
        src_ref=rows.at[outer], dst_ref=halo, send_sem=ss5, recv_sem=rs5,
        device_id={"range": 1 - r}, device_id_type=MESH,
    )
    edge.start()

    def wait_bins(d, carry):
        s = lax.rem(q + d, NQ)

        @pl.when(s != outer)
        def _():
            from_bins(s).wait_recv()

        return carry

    lax.fori_loop(1, NQ, wait_bins, 0)

    def flat(x):
        return x.astype(F32).reshape(64, 128)

    def place(i, tile, x):
        win[i, :, tile * 128 : (tile + 1) * 128] = x

    for i in range(16):
        x0, x1 = flat(rows[2 * i]).astype(BF16), flat(rows[2 * i + 1]).astype(BF16)
        place(i, 1, x0)
        place(i, 2, x1)
        if i > 0:
            place(i - 1, 3, x0)
        if i < 15:
            place(i + 1, 0, x1)
    noise[...] = jnp.dot(win[...].reshape(1024, 512), band[...], preferred_element_type=F32)

    def detect(t, more):
        i, e = t // 2, t % 2
        level = noise[i * 64 : (i + 1) * 64, e * 128 : (e + 1) * 128] + more
        got = flat(rows[t]) / (level * (1.0 / (2 * TRAIN)) + NOISE_FLOOR)
        for f in range(8):
            turned[t, pl.ds(f, 8, stride=8), :] = got[f * 8 : f * 8 + 8]
        out[:, t * 128 : (t + 1) * 128] = turned[t].astype(out.dtype)

    for t in range(1, 31):
        detect(t, 0.0)
    edge.wait()
    beside, right = flat(halo[...]), r.astype(F32)
    low = jnp.dot((beside * right).astype(BF16), band[0:128, 0:128], preferred_element_type=F32)
    high = jnp.dot((beside * (1.0 - right)).astype(BF16), band[384:512, 128:256], preferred_element_type=F32)
    detect(0, low)
    detect(31, high)
    for i in range(NQ - 1):
        to_bins(i).wait_send()


def shards(signal, steering, spectrum):
    lanes, twist = lane_tables()
    dma = pltpu.SemaphoreType.DMA
    scratch = [
        pltpu.VMEM((2, 16, 8, 4096), BF16),
        pltpu.VMEM((2, 32, 64), BF16),
        pltpu.VMEM((2, 8192), F32),
        pltpu.VMEM((2, 256, 256), BF16),
        pltpu.VMEM((2, 64, 128), F32),
        pltpu.VMEM((64, 128), BF16),
        pltpu.VMEM((64, 128), F32),
        pltpu.VMEM((128, 128), F32),
        pltpu.VMEM((2, 512, 128), F32),
        pltpu.VMEM((2, 512, 128), F32),
        pltpu.VMEM((512, 256), BF16),
        pltpu.VMEM((32, 256, 128), F32),
        pltpu.VMEM((8, 8, 4, 32, 128), BF16),
        pltpu.VMEM((8, 8, 4, 32, 128), BF16),
        pltpu.VMEM((2, 8, 64, 128), F32),
        pltpu.VMEM((4, 64, 16, 128), F32),
        pltpu.VMEM((64, 16, 128), F32),
        pltpu.VMEM((512, 256), BF16),
        pltpu.VMEM((512, 256), F32),
        pltpu.VMEM((4, 2, 32, 16, 128), BF16),
        pltpu.VMEM((4, 2, 32, 16, 128), BF16),
        pltpu.VMEM((2, 32, 16, 128), BF16),
        pltpu.VMEM((8, 32, 16, 128), BF16),
        pltpu.VMEM((256, 16, 128), F32),
        pltpu.VMEM((256, 8, 128), BF16),
        pltpu.VMEM((32, 8, 8, 128), BF16),
        pltpu.VMEM((8, 8, 128), BF16),
        pltpu.VMEM((16, 64, 512), BF16),
        pltpu.VMEM((1024, 256), F32),
        pltpu.VMEM((32, 64, 128), F32),
        dma((5,)),
        dma((7, CHUNKS)), dma((7, CHUNKS)),
        dma((4,)), dma((4,)),
        dma((7,)), dma((7,)),
        dma((32,)), dma((32,)),
        dma, dma,
        dma, dma,
    ]
    got = pl.pallas_call(
        kernel,
        out_shape=jax.ShapeDtypeStruct((64, 4096), BF16),
        in_specs=[pl.BlockSpec(memory_space=pl.ANY)] * 5,
        out_specs=pl.BlockSpec(memory_space=pltpu.VMEM),
        scratch_shapes=scratch,
        compiler_params=pltpu.CompilerParams(collective_id=0, has_side_effects=True, vmem_limit_bytes=60 * 2**20),
        name="radar",
    )(signal, steering, spectrum, jnp.asarray(lanes, BF16), jnp.asarray(twist, F32))
    return got.reshape(8, 8, 4096).astype(F32)


def solution(mesh):
    return jax.shard_map(
        shards,
        mesh=mesh,
        in_specs=(P(None, "chan", "pulse", "range"), P(), P()),
        out_specs=P("chan", "pulse", "range"),
        check_vma=False,
    )
```

time: 118 us -> 99 us (0.84)
  Pallas kernels: 111 us -> 96.8 us
  local copies, waits for them, and re-layouts: 5.45 us -> 0 us
    pallas_call x1, Pallas kernels: 111 us -> 96.8 us  [shards(): pl.pallas_call(kernel, out_shape=jax.ShapeDtypeStruct((64, 4096), BF16),...]
    unnamed x1 -> x0, local copies, waits for them, and re-layouts: 2.27 us -> none
    convert_element_type x0 -> x1, other arithmetic: none -> 2.08 us  [shards(): return got.reshape(8, 8, 4096).astype(F32)]
    mul x2 -> x0, local copies, waits for them, and re-layouts: 1.55 us -> none  [shards(): spectrum.reshape(2, 128, 8, 8).transpose(0, 3, 2, 1).reshape(2, 64, 128)]
where the time goes in v1:
time: 99 us; the launch traced here: 98.9 us
  Pallas kernels  96.8 us (98%)
  other arithmetic  2.08 us (2%)
    pallas_call x1, Pallas kernels, shards(): pl.pallas_call(kernel, out_shape=jax.ShapeDtypeStruct((64, 4096), BF16),...  96.8 us
    convert_element_type x1, other arithmetic, shards(): return got.reshape(8, 8, 4096).astype(F32)  2.08 us

profile of v1, /device:TPU:1, one launch (start us, length us, event | category | flops | bytes accessed | tf_op | source)
XLA Modules:
  0.0 98.9 jit_solution(1933507093356887564)
XLA Ops:
  0.0 96.8 %radar.1 = bf16[64,4096]{1,0:T(8,128)(2,1)} custom-call(bf16[2,16,8,4096]{3,2,1,0:T(8,128)(2,1)} %sig_hbm.1, bf16[2,32,64]{2,1,0:T(8,128)(2,1)} %steer_hbm.1, f32[2,8192]{1,0:T(2,128)} %spec_hbm.1, bf16[2,256,256]{2,1,0:T(8,128)(2,1)} %constant.4.clone.lanes_hbm, f32[2,64,128]{2,1,0:T(8,128)} %constant.5.clone.twist_hbm), custom_call_target="tpu_custom_call" | custom-call | tf_op jit(solution)/shard_map/radar/pallas_call | solution.py:431
  96.8 2.1 %bitcast_convert_fusion = f32[8,8,4096]{2,1,0:T(8,128)} fusion(bf16[64,4096]{1,0:T(8,128)(2,1)} %radar.1), kind=kLoop, calls=%fused_computation | loop fusion | flops 262144 | bytes 1572864 | tf_op jit(solution)/shard_map/convert_element_type | solution.py:440

commit v2 on v1

v2 whole, which is shorter than its diff:
```python
import math

import jax
import jax.numpy as jnp
import numpy as np
from jax import lax
from jax.experimental import pallas as pl
from jax.experimental.pallas import tpu as pltpu
from jax.sharding import PartitionSpec as P

F32, BF16 = jnp.float32, jnp.bfloat16
MESH = pl.DeviceIdType.MESH
GUARD, TRAIN, NOISE_FLOOR = 4, 16, 0.25
NZ, NQ = 8, 32
HOPS = (4, 3, -3, 2, -2, 1, -1)
GROUPS = (2, 1, 3, 0)
NEAR_LAST = (10, 6, 9, 11, 14, 2, 8, 5, 7, 13, 15, 1, 3, 4, 12)
CHUNKS = 4


def times(v, angle_num, period, sign):
    k = angle_num % period
    if k == 0:
        return v
    re, im = v
    if 4 * k == period:
        return (-im, re) if sign > 0 else (im, -re)
    if 2 * k == period:
        return (-re, -im)
    if 4 * k == 3 * period:
        return (im, -re) if sign > 0 else (-im, re)
    c = math.cos(2 * math.pi * k / period)
    s = sign * math.sin(2 * math.pi * k / period)
    return (re * c - im * s, re * s + im * c)


def dft(xs, sign):
    n = len(xs)
    if n == 1:
        return xs
    even, odd = dft(xs[0::2], sign), dft(xs[1::2], sign)
    odd = [times(v, k, n, sign) for k, v in enumerate(odd)]
    plus = [(a[0] + b[0], a[1] + b[1]) for a, b in zip(even, odd)]
    minus = [(a[0] - b[0], a[1] - b[1]) for a, b in zip(even, odd)]
    return plus + minus


def pair(x):
    x = x.astype(F32)
    return (x[:8], x[8:])


def joined(v):
    return jnp.concatenate(v, axis=0)


def lane_tables():
    n = np.arange(128)
    k2 = 2 * (n % 64) + n // 64
    ang = 2 * np.pi * (np.outer(n, k2) % 128) / 128
    c, s = np.cos(ang), np.sin(ang)
    ahead = np.block([[c, -s], [s, c]])
    back = np.block([[c.T, s.T], [-s.T, c.T]])
    k1 = (np.arange(8)[:, None] + 8 * np.arange(8)[None, :]).reshape(-1)
    turn = 2 * np.pi * np.outer(k1, n) / 8192
    twist = np.stack([np.cos(turn), -np.sin(turn)])
    return np.stack([ahead, back]), twist


def spread(rows):
    return jnp.broadcast_to(rows[:, None, :], (8, 8, 128)).reshape(64, 128)


def zdev(z):
    return {"chan": z // 2, "range": lax.rem(z, 2)}


def kernel(
    sig_hbm, steer_hbm, spec_hbm, lanes_hbm, twist_hbm, rows_hbm, halo,
    sig, steer, spec, lanes, twist, wmat, rowed, turned_resp, resp, tw,
    wide, send, recv, formed, mid, mid2, lhs, prod, comp, crossed, early, cols, dmid, power, rows,
    loads, parts, ss1, rs1, ss2, rs2, ss3, rs3, ss4, rs4, ss5, rs5, ss6, rs6, ss7, rs7, stores,
):
    c, q, r = lax.axis_index("chan"), lax.axis_index("pulse"), lax.axis_index("range")
    me = c * 2 + r
    bar = pltpu.get_barrier_semaphore()
    for d in range(1, NZ):
        pl.semaphore_signal(bar, inc=1, device_id=zdev(lax.rem(me + d, NZ)), device_id_type=MESH)

    def greet(d, carry):
        pl.semaphore_signal(bar, inc=1, device_id={"pulse": lax.rem(q + d, NQ)}, device_id_type=MESH)
        return carry

    lax.fori_loop(1, NQ, greet, 0)
    fetched = [
        pltpu.make_async_copy(a, b, loads.at[i])
        for i, (a, b) in enumerate(
            [(steer_hbm, steer), (spec_hbm, spec), (lanes_hbm, lanes), (twist_hbm, twist)]
        )
    ]
    per = 8 // CHUNKS

    def part_copy(part, a):
        at = (slice(None), slice(None), slice(None), pl.ds((8 * a + part * per) * 128, per * 128))
        return pltpu.make_async_copy(sig_hbm.at[at], sig.at[at], parts.at[part, a])

    for part in range(CHUNKS):
        for a in range(4):
            part_copy(part, a).start()
    for copy in fetched:
        copy.start()

    def widen(part):
        for a in range(4):
            part_copy(part, a).wait()
        for a in range(4):
            for b in range(part * per, (part + 1) * per):
                t = 8 * a + b
                wide[t] = sig[:, :, :, t * 128 : (t + 1) * 128].astype(F32).reshape(256, 128)

    def take_pulse(j, part, into, at):
        for b in range(part * per, (part + 1) * per):
            for a in range(4):
                into[at, b, a] = wide[8 * a + b, pl.ds(j, 32, stride=8), :].astype(BF16)

    def hop(k, part):
        t = lax.rem(me + HOPS[k] + NZ, NZ)
        mine = pl.ds(part * per, per)
        return t, pltpu.make_async_remote_copy(
            src_ref=send.at[t, mine], dst_ref=recv.at[me, mine], send_sem=ss1.at[k, part], recv_sem=rs1.at[k, part],
            device_id=zdev(t), device_id_type=MESH,
        )

    for part in range(CHUNKS):
        widen(part)
        for k in range(7):
            t, copy = hop(k, part)
            take_pulse(t, part, send, t)
            if k == 0 and part == 0:
                pl.semaphore_wait(bar, NZ - 1 + NQ - 1)
            copy.start()
    for part in range(CHUNKS):
        take_pulse(me, part, recv, me)

    for copy in fetched:
        copy.wait()
    wr, wi = steer[0].astype(F32), steer[1].astype(F32)
    wmat[0:32] = jnp.concatenate([wr, -wi], axis=1).astype(BF16)
    wmat[32:64] = jnp.concatenate([wi, wr], axis=1).astype(BF16)
    for i in range(2):
        for m in range(64):
            rowed[m : m + 1] = spec[i : i + 1, m * 128 : (m + 1) * 128]
        a = rowed[...] * (1.0 / 8192)
        both = jnp.concatenate([a, jnp.concatenate([a[:, 64:], a[:, :64]], axis=1)], axis=0)
        turned_resp[...] = jnp.transpose(both)
        for ka in range(8):
            resp[i, ka * 64 : ka * 64 + 64] = spread(turned_resp[pl.ds(ka, 8, stride=8), :])
            tw[i, ka * 64 : ka * 64 + 64] = spread(twist[i, ka * 8 : ka * 8 + 8])

    def front(b):
        now = b % 2
        for half in range(2):
            for a in (0, 2):
                blocks = []
                for e in range(2):
                    tiles = [recv[2 * cc + half, b, a + e] for cc in range(4)]
                    blocks.append(jnp.concatenate([t[:16] for t in tiles] + [t[16:] for t in tiles], axis=0))
                got = jnp.dot(wmat[...], jnp.concatenate(blocks, axis=1), preferred_element_type=F32)
                got = got.astype(BF16).astype(F32)
                for e in range(2):
                    formed[now, half * 4 + a + e] = got[:, e * 128 : (e + 1) * 128]
        for g in range(4):
            xs = [(formed[now, a, 8 * g : 8 * g + 8], formed[now, a, 32 + 8 * g : 40 + 8 * g]) for a in range(8)]
            ys = dft(xs, -1)
            for ka in range(8):
                mid[g, b * 8 + ka] = joined(times(ys[ka], b * ka, 64, -1))

    for part in range(CHUNKS):
        for k in range(7):
            hop(k, part)[1].wait_recv()
        for b in range(part * per, (part + 1) * per):
            front(b)

    def filter_group(g):
        for ka in range(8):
            here = slice(ka * 64, ka * 64 + 64)
            xs = dft([pair(mid[g, b * 8 + ka]) for b in range(8)], -1)
            tr, ti = tw[0, here], tw[1, here]
            re = jnp.concatenate([v[0] for v in xs], axis=0)
            im = jnp.concatenate([v[1] for v in xs], axis=0)
            lhs[here, 0:128] = (re * tr - im * ti).astype(BF16)
            lhs[here, 128:256] = (re * ti + im * tr).astype(BF16)
        prod[...] = jnp.dot(lhs[...], lanes[0], preferred_element_type=F32)
        for ka in range(8):
            here = slice(ka * 64, ka * 64 + 64)
            hr, hi = resp[0, here], resp[1, here]
            re, im = prod[here, 0:128], prod[here, 128:256]
            lhs[here, 0:128] = (re * hr - im * hi).astype(BF16)
            lhs[here, 128:256] = (re * hi + im * hr).astype(BF16)
        prod[...] = jnp.dot(lhs[...], lanes[1], preferred_element_type=F32)
        for ka in range(8):
            here = slice(ka * 64, ka * 64 + 64)
            tr, ti = tw[0, here], tw[1, here]
            re, im = prod[here, 0:128], prod[here, 128:256]
            re, im = re * tr + im * ti, im * tr - re * ti
            ys = dft([(re[8 * kb : 8 * kb + 8], im[8 * kb : 8 * kb + 8]) for kb in range(8)], 1)
            for b in range(8):
                mid2[b * 8 + ka] = joined(times(ys[b], b * ka, 64, 1))
        for b in range(8):
            xs = dft([pair(mid2[b * 8 + ka]) for ka in range(8)], 1)
            for a in range(8):
                n1 = 8 * a + b
                t = n1 if n1 < 32 else 63 - n1
                comp[g, 1 - t % 2, n1 // 32, t // 2] = joined(xs[a]).astype(BF16)

    k, i0 = 1 - lax.rem(q, 2), q // 2

    def chip(i, core):
        x, y = i0 // 4, lax.rem(i0, 4)
        return (lax.rem(x + i // 4, 4) * 4 + lax.rem(y + i % 4, 4)) * 2 + 1 - core

    def along(step, e, src, dst, ss, rs):
        g, rr = lax.rem(c + GROUPS[step], 4), lax.rem(r + e, 2)
        return pltpu.make_async_remote_copy(
            src_ref=src(g, rr), dst_ref=dst, send_sem=ss.at[step, e], recv_sem=rs.at[step, e],
            device_id={"chan": g, "range": rr}, device_id_type=MESH,
        )

    def first_set(step, e):
        return along(step, e, lambda g, rr: comp.at[g, 0, rr], early.at[me], ss3, rs3)

    def second_set(step, e):
        return along(step, e, lambda g, rr: crossed.at[g, rr], cols.at[me], ss7, rs7)

    def cross(g, i):
        t = chip(i, 1)
        return pltpu.make_async_remote_copy(
            src_ref=comp.at[g, 1, :, t // 2], dst_ref=crossed.at[g, :, q],
            send_sem=ss2.at[g, 0 if i else 1], recv_sem=rs2.at[g],
            device_id={"pulse": t}, device_id_type=MESH,
        )

    def forward(cs, i):
        t = chip(i, 0)
        pick = pl.ds(2 * cs, 2)
        return pltpu.make_async_remote_copy(
            src_ref=early.at[pick, t // 2], dst_ref=cols.at[pick, q], send_sem=ss6.at[0 if i else 1], recv_sem=rs6,
            device_id={"pulse": t}, device_id_type=MESH,
        )

    def send_group(step):
        g = lax.rem(c + GROUPS[step], 4)
        for e in range(2):
            if GROUPS[step] or e:
                first_set(step, e).start()
        for i in NEAR_LAST:
            cross(g, i).start()

        @pl.when(k == 0)
        def _():
            cross(g, 0).start()

        @pl.when(k == 1)
        def _():
            for rr in range(2):
                crossed[g, rr, q] = comp[g, 1, rr, i0]

    for step in range(4):
        filter_group(lax.rem(c + GROUPS[step], 4))
        send_group(step)
    for i in range(16):
        early[me, i] = comp[c, 0, r, i]

    def second_go(step):
        @pl.when(k == 1)
        def _():
            g = lax.rem(c + GROUPS[step], 4)
            whole = crossed.at[g, :, pl.ds(0, NQ - 1)]
            pltpu.make_async_copy(whole, whole, rs2.at[g]).wait()
            for e in range(2):
                if GROUPS[step] or e:
                    second_set(step, e).start()

    def first_go(step):
        cs = lax.rem(c - GROUPS[step] + 4, 4)
        for e in range(2):
            if GROUPS[step] or e:
                first_set(step, e).wait_recv()
        for i in NEAR_LAST:
            forward(cs, i).start()

        @pl.when(k == 1)
        def _():
            forward(cs, 0).start()

        @pl.when(k == 0)
        def _():
            for e in range(2):
                cols[2 * cs + e, q] = early[2 * cs + e, i0]

    second_go(0)
    second_go(1)
    first_go(0)
    second_go(2)
    first_go(1)
    second_go(3)
    first_go(2)
    first_go(3)

    @pl.when(k == 1)
    def _():
        def keep(t, carry):
            cols[me, t] = crossed[c, r, t]
            return carry

        lax.fori_loop(0, NQ, keep, 0, unroll=4)
        for step in range(4):
            for e in range(2):
                if GROUPS[step] or e:
                    second_set(step, e).wait_recv()

    @pl.when(k == 0)
    def _():
        whole = cols.at[:, pl.ds(0, NQ - 1)]
        pltpu.make_async_copy(whole, whole, rs6).wait()

    for b in range(16):
        ps = [16 * a + b for a in range(16)]
        ys = dft([pair(cols[p % 8, p // 8]) for p in ps], -1)
        for fa in range(16):
            dmid[b * 16 + fa] = joined(times(ys[fa], b * fa, 256, -1))
    def to_bins(core, i):
        t = lax.rem(i0 // 4 + i // 4, 4) * 8 + lax.rem(i0 + i, 4) * 2 + core
        return pltpu.make_async_remote_copy(
            src_ref=power.at[pl.ds(t * 8, 8)], dst_ref=rows.at[q], send_sem=ss4.at[core, i], recv_sem=rs4.at[q],
            device_id={"pulse": t}, device_id_type=MESH,
        )

    def from_bins(s):
        return pltpu.make_async_remote_copy(
            src_ref=power.at[pl.ds(s * 8, 8)], dst_ref=rows.at[s], send_sem=ss4.at[0, 0], recv_sem=rs4.at[s],
            device_id={"pulse": s}, device_id_type=MESH,
        )

    for core in range(2):
        for fa in range(core * 8, core * 8 + 8):
            xs = dft([pair(dmid[b * 16 + fa]) for b in range(16)], -1)
            for fb in range(16):
                re, im = xs[fb]
                power[fa + 16 * fb] = ((re * re + im * im) * (1.0 / 256)).astype(BF16)
        for i in NEAR_LAST:
            to_bins(core, i).start()

        @pl.when(lax.rem(q, 2) == 1 - core)
        def _():
            to_bins(core, 0).start()

    for part in range(CHUNKS):
        for h in range(7):
            hop(h, part)[1].wait_send()
    for step in range(4):
        for e in range(2):
            if GROUPS[step] or e:
                first_set(step, e).wait_send()
    for g in range(4):
        whole = comp.at[g, 1, :, pl.ds(0, 15)]
        pltpu.make_async_copy(whole, whole, ss2.at[g, 0]).wait()
    whole = early.at[:, pl.ds(0, 15)]
    pltpu.make_async_copy(whole, whole, ss6.at[0]).wait()

    @pl.when(k == 0)
    def _():
        for g in range(4):
            whole = comp.at[g, 1, :, 0]
            pltpu.make_async_copy(whole, whole, ss2.at[g, 1]).wait()

    @pl.when(k == 1)
    def _():
        whole = early.at[:, 0]
        pltpu.make_async_copy(whole, whole, ss6.at[1]).wait()
        for step in range(4):
            for e in range(2):
                if GROUPS[step] or e:
                    second_set(step, e).wait_send()

    rows[q] = power[pl.ds(q * 8, 8)]
    outer = NQ - 1

    def store(s):
        return pltpu.make_async_copy(rows.at[s], rows_hbm.at[s], stores)

    store(q).start()

    @pl.when(q != outer)
    def _():
        from_bins(outer).wait_recv()
        store(outer).start()

    edge = pltpu.make_async_remote_copy(
        src_ref=rows.at[outer], dst_ref=halo, send_sem=ss5, recv_sem=rs5,
        device_id={"range": 1 - r}, device_id_type=MESH,
    )
    edge.start()

    def wait_bins(d, carry):
        s = lax.rem(q + d, NQ)

        @pl.when(s != outer)
        def _():
            from_bins(s).wait_recv()
            store(s).start()

        return carry

    lax.fori_loop(1, NQ, wait_bins, 0)

    edge.wait()
    pltpu.make_async_copy(rows, rows_hbm, stores).wait()
    for core in range(2):
        for i in NEAR_LAST:
            to_bins(core, i).wait_send()

        @pl.when(lax.rem(q, 2) == 1 - core)
        def _():
            to_bins(core, 0).wait_send()


def band_table():
    gap = np.abs(np.arange(512)[:, None] - (128 + np.arange(256)[None, :]))
    return ((gap > GUARD) & (gap <= GUARD + TRAIN)).astype(np.float32)


def window(rows, halo, band, out_hbm, win, noise, turned, out, done):
    r = lax.axis_index("range")
    right = r.astype(F32)

    def tile(t):
        return rows[t + r * (31 - 2 * t)].astype(F32).reshape(64, 128)

    def place(i, at, x):
        win[i, :, at * 128 : (at + 1) * 128] = x

    beside = halo[...].astype(F32).reshape(64, 128)
    place(0, 0, (beside * right).astype(BF16))
    place(15, 3, (beside * (1.0 - right)).astype(BF16))
    for i in range(16):
        x0, x1 = tile(2 * i).astype(BF16), tile(2 * i + 1).astype(BF16)
        place(i, 1, x0)
        place(i, 2, x1)
        if i > 0:
            place(i - 1, 3, x0)
        if i < 15:
            place(i + 1, 0, x1)
    copies = []
    for part in range(4):
        here = slice(part * 4, part * 4 + 4)
        noise[part] = jnp.dot(win[here].reshape(256, 512), band[...], preferred_element_type=F32)
        for t in range(part * 8, part * 8 + 8):
            i, e = t // 2 - part * 4, t % 2
            level = noise[part, i * 64 : (i + 1) * 64, e * 128 : (e + 1) * 128]
            got = tile(t) / (level * (1.0 / (2 * TRAIN)) + NOISE_FLOOR)
            for f in range(8):
                turned[t, pl.ds(f, 8, stride=8), :] = got[f * 8 : f * 8 + 8]
            out[:, t * 128 : (t + 1) * 128] = turned[t]
        lanes = pl.ds(part * 1024, 1024)
        copies.append(pltpu.make_async_copy(out.at[:, lanes], out_hbm.at[:, lanes], done.at[part]))
        copies[-1].start()
    for copy in copies:
        copy.wait()


def shards(signal, steering, spectrum):
    lanes, twist = lane_tables()
    dma = pltpu.SemaphoreType.DMA
    hbm = pl.BlockSpec(memory_space=pl.ANY)
    scratch = [
        pltpu.VMEM((2, 16, 8, 4096), BF16),
        pltpu.VMEM((2, 32, 64), BF16),
        pltpu.VMEM((2, 8192), F32),
        pltpu.VMEM((2, 256, 256), BF16),
        pltpu.VMEM((2, 64, 128), F32),
        pltpu.VMEM((64, 128), BF16),
        pltpu.VMEM((64, 128), F32),
        pltpu.VMEM((128, 128), F32),
        pltpu.VMEM((2, 512, 128), F32),
        pltpu.VMEM((2, 512, 128), F32),
        pltpu.VMEM((32, 256, 128), F32),
        pltpu.VMEM((8, 8, 4, 32, 128), BF16),
        pltpu.VMEM((8, 8, 4, 32, 128), BF16),
        pltpu.VMEM((2, 8, 64, 128), F32),
        pltpu.VMEM((4, 64, 16, 128), F32),
        pltpu.VMEM((64, 16, 128), F32),
        pltpu.VMEM((512, 256), BF16),
        pltpu.VMEM((512, 256), F32),
        pltpu.VMEM((4, 2, 2, 16, 16, 128), BF16),
        pltpu.VMEM((4, 2, 32, 16, 128), BF16),
        pltpu.VMEM((8, 16, 16, 128), BF16),
        pltpu.VMEM((8, 32, 16, 128), BF16),
        pltpu.VMEM((256, 16, 128), F32),
        pltpu.VMEM((256, 8, 128), BF16),
        pltpu.VMEM((32, 8, 8, 128), BF16),
        dma((4,)), dma((CHUNKS, 4)),
        dma((7, CHUNKS)), dma((7, CHUNKS)),
        dma((4, 2)), dma((4,)),
        dma((4, 2)), dma((4, 2)),
        dma((2, 16)), dma((32,)),
        dma, dma,
        dma((2,)), dma,
        dma((4, 2)), dma((4, 2)),
        dma,
    ]
    rows, halo = pl.pallas_call(
        kernel,
        out_shape=[jax.ShapeDtypeStruct((32, 8, 8, 128), BF16), jax.ShapeDtypeStruct((8, 8, 128), BF16)],
        in_specs=[hbm] * 5,
        out_specs=[hbm, hbm],
        scratch_shapes=scratch,
        compiler_params=pltpu.CompilerParams(collective_id=0, has_side_effects=True, vmem_limit_bytes=60 * 2**20),
        name="radar",
    )(signal, steering, spectrum, jnp.asarray(lanes, BF16), jnp.asarray(twist, F32))
    got = pl.pallas_call(
        window,
        out_shape=jax.ShapeDtypeStruct((64, 4096), F32),
        in_specs=[pl.BlockSpec(memory_space=pltpu.VMEM)] * 3,
        out_specs=hbm,
        scratch_shapes=[
            pltpu.VMEM((16, 64, 512), BF16),
            pltpu.VMEM((4, 256, 256), F32),
            pltpu.VMEM((32, 64, 128), F32),
            pltpu.VMEM((64, 4096), F32),
            dma((4,)),
        ],
        compiler_params=pltpu.CompilerParams(vmem_limit_bytes=60 * 2**20),
        name="window",
    )(rows, halo, jnp.asarray(band_table(), BF16))
    return got.reshape(8, 8, 4096)


def solution(mesh):
    return jax.shard_map(
        shards,
        mesh=mesh,
        in_specs=(P(None, "chan", "pulse", "range"), P(), P()),
        out_specs=P("chan", "pulse", "range"),
        check_vma=False,
    )
```

time: 99 us -> 95.5 us (0.965)
  other arithmetic: 2.08 us -> 0 us
  Pallas kernels: 96.8 us -> 95.3 us
    convert_element_type x1 -> x0, other arithmetic: 2.08 us -> none  [shards(): return got.reshape(8, 8, 4096).astype(F32)]
    pallas_call x1 -> x2, Pallas kernels: 96.8 us -> 95.3 us  [the longest x1 92.8 us: shards(): pl.pallas_call(kernel, out_shape=[jax.ShapeDtypeStruct((32, 8, 8, 128), B...]
where the time goes in v2:
time: 95.5 us; the launch traced here: 95.3 us
  Pallas kernels  95.3 us (100%)
    pallas_call x1, Pallas kernels, shards(): pl.pallas_call(kernel, out_shape=[jax.ShapeDtypeStruct((32, 8, 8, 128), B...  92.8 us
    pallas_call x1, Pallas kernels, shards(): pl.pallas_call(window, out_shape=jax.ShapeDtypeStruct((64, 4096), F32), i...  2.55 us

profile of v2, /device:TPU:1, one launch (start us, length us, event | category | flops | bytes accessed | tf_op | source)
XLA Modules:
  0.0 95.3 jit_solution(17918212226778255244)
XLA Ops:
  0.0 92.8 %radar.1 = (bf16[32,8,8,128]{3,2,1,0:T(8,128)(2,1)}, bf16[8,8,128]{2,1,0:T(8,128)(2,1)}) custom-call(bf16[2,16,8,4096]{3,2,1,0:T(8,128)(2,1)} %sig_hbm.1, bf16[2,32,64]{2,1,0:T(8,128)(2,1)} %steer_hbm.1, f32[2,8192]{1,0:T(2,128)} %spec_hbm.1, bf16[2,256,256]{2,1,0:T(8,128)(2,1)} %constant.6.clone.lanes_hbm, f32[2,64,128]{2,1,0:T(8,128)} %constant.7.clone.twist_hbm), custom_call_target="tpu_custom_call" | custom-call | tf_op jit(solution)/shard_map/radar/pallas_call | solution.py:512
  92.8 2.5 %window.1 = f32[64,4096]{1,0:T(8,128)} custom-call(bf16[32,8,8,128]{3,2,1,0:T(8,128)(2,1)} %get-tuple-element.7.rows, bf16[8,8,128]{2,1,0:T(8,128)(2,1)} %get-tuple-element.8.halo, bf16[512,256]{1,0:T(8,128)(2,1)} %constant.8.clone.band), custom_call_target="tpu_custom_call" | custom-call | tf_op jit(solution)/shard_map/window/pallas_call | solution.py:521

commit v3 on v2

--- a/solution.py
+++ b/solution.py
@@ -14,8 +14,8 @@
 NZ, NQ = 8, 32
 HOPS = (4, 3, -3, 2, -2, 1, -1)
 GROUPS = (2, 1, 3, 0)
-NEAR_LAST = (10, 6, 9, 11, 14, 2, 8, 5, 7, 13, 15, 1, 3, 4, 12)
-CHUNKS = 4
+NEAR_LAST = (10, 6, 14, 9, 11, 5, 15, 7, 13, 8, 2, 4, 12, 1, 3)
+CHUNKS = 8
 
 
 def times(v, angle_num, period, sign):
@@ -76,9 +76,9 @@
 
 
 def kernel(
-    sig_hbm, steer_hbm, spec_hbm, lanes_hbm, twist_hbm, rows_hbm, halo,
+    sig_hbm, steer_hbm, spec_hbm, lanes_hbm, twist_hbm, rows, halo,
     sig, steer, spec, lanes, twist, wmat, rowed, turned_resp, resp, tw,
-    wide, send, recv, formed, mid, mid2, lhs, prod, comp, crossed, early, cols, dmid, power, rows,
+    wide, send, recv, formed, mid, mid2, lhs, prod, comp, crossed, early, cols, dmid, power,
     loads, parts, ss1, rs1, ss2, rs2, ss3, rs3, ss4, rs4, ss5, rs5, ss6, rs6, ss7, rs7, stores,
 ):
     c, q, r = lax.axis_index("chan"), lax.axis_index("pulse"), lax.axis_index("range")
@@ -100,9 +100,12 @@
     ]
     per = 8 // CHUNKS
 
+    def drain(ref, sem):
+        pltpu.make_async_copy(ref, ref, sem).wait()
+
     def part_copy(part, a):
         at = (slice(None), slice(None), slice(None), pl.ds((8 * a + part * per) * 128, per * 128))
-        return pltpu.make_async_copy(sig_hbm.at[at], sig.at[at], parts.at[part, a])
+        return pltpu.make_async_copy(sig_hbm.at[at], sig.at[at], parts.at[part])
 
     for part in range(CHUNKS):
         for a in range(4):
@@ -111,8 +114,7 @@
         copy.start()
 
     def widen(part):
-        for a in range(4):
-            part_copy(part, a).wait()
+        drain(sig.at[:, :, :, pl.ds(0, 4 * per * 128)], parts.at[part])
         for a in range(4):
             for b in range(part * per, (part + 1) * per):
                 t = 8 * a + b
@@ -127,7 +129,7 @@
         t = lax.rem(me + HOPS[k] + NZ, NZ)
         mine = pl.ds(part * per, per)
         return t, pltpu.make_async_remote_copy(
-            src_ref=send.at[t, mine], dst_ref=recv.at[me, mine], send_sem=ss1.at[k, part], recv_sem=rs1.at[k, part],
+            src_ref=send.at[t, mine], dst_ref=recv.at[me, mine], send_sem=ss1, recv_sem=rs1.at[part],
             device_id=zdev(t), device_id_type=MESH,
         )
 
@@ -176,8 +178,7 @@
                 mid[g, b * 8 + ka] = joined(times(ys[ka], b * ka, 64, -1))
 
     for part in range(CHUNKS):
-        for k in range(7):
-            hop(k, part)[1].wait_recv()
+        drain(recv.at[pl.ds(0, 7), pl.ds(0, per)], rs1.at[part])
         for b in range(part * per, (part + 1) * per):
             front(b)
 
@@ -222,12 +223,12 @@
     def along(step, e, src, dst, ss, rs):
         g, rr = lax.rem(c + GROUPS[step], 4), lax.rem(r + e, 2)
         return pltpu.make_async_remote_copy(
-            src_ref=src(g, rr), dst_ref=dst, send_sem=ss.at[step, e], recv_sem=rs.at[step, e],
+            src_ref=src(g, rr), dst_ref=dst, send_sem=ss, recv_sem=rs,
             device_id={"chan": g, "range": rr}, device_id_type=MESH,
         )
 
     def first_set(step, e):
-        return along(step, e, lambda g, rr: comp.at[g, 0, rr], early.at[me], ss3, rs3)
+        return along(step, e, lambda g, rr: comp.at[g, 0, rr], early.at[me], ss3, rs3.at[step])
 
     def second_set(step, e):
         return along(step, e, lambda g, rr: crossed.at[g, rr], cols.at[me], ss7, rs7)
@@ -236,7 +237,7 @@
         t = chip(i, 1)
         return pltpu.make_async_remote_copy(
             src_ref=comp.at[g, 1, :, t // 2], dst_ref=crossed.at[g, :, q],
-            send_sem=ss2.at[g, 0 if i else 1], recv_sem=rs2.at[g],
+            send_sem=ss2, recv_sem=rs2.at[g],
             device_id={"pulse": t}, device_id_type=MESH,
         )
 
@@ -244,7 +245,7 @@
         t = chip(i, 0)
         pick = pl.ds(2 * cs, 2)
         return pltpu.make_async_remote_copy(
-            src_ref=early.at[pick, t // 2], dst_ref=cols.at[pick, q], send_sem=ss6.at[0 if i else 1], recv_sem=rs6,
+            src_ref=early.at[pick, t // 2], dst_ref=cols.at[pick, q], send_sem=ss6, recv_sem=rs6,
             device_id={"pulse": t}, device_id_type=MESH,
         )
 
@@ -275,17 +276,14 @@
         @pl.when(k == 1)
         def _():
             g = lax.rem(c + GROUPS[step], 4)
-            whole = crossed.at[g, :, pl.ds(0, NQ - 1)]
-            pltpu.make_async_copy(whole, whole, rs2.at[g]).wait()
+            drain(crossed.at[g, :, pl.ds(0, NQ - 1)], rs2.at[g])
             for e in range(2):
                 if GROUPS[step] or e:
                     second_set(step, e).start()
 
     def first_go(step):
         cs = lax.rem(c - GROUPS[step] + 4, 4)
-        for e in range(2):
-            if GROUPS[step] or e:
-                first_set(step, e).wait_recv()
+        drain(early.at[pl.ds(0, 2 if GROUPS[step] else 1)], rs3.at[step])
         for i in NEAR_LAST:
             forward(cs, i).start()
 
@@ -314,15 +312,11 @@
             return carry
 
         lax.fori_loop(0, NQ, keep, 0, unroll=4)
-        for step in range(4):
-            for e in range(2):
-                if GROUPS[step] or e:
-                    second_set(step, e).wait_recv()
+        drain(cols.at[pl.ds(0, NZ - 1)], rs7)
 
     @pl.when(k == 0)
     def _():
-        whole = cols.at[:, pl.ds(0, NQ - 1)]
-        pltpu.make_async_copy(whole, whole, rs6).wait()
+        drain(cols.at[:, pl.ds(0, NQ - 1)], rs6)
 
     for b in range(16):
         ps = [16 * a + b for a in range(16)]
@@ -332,14 +326,8 @@
     def to_bins(core, i):
         t = lax.rem(i0 // 4 + i // 4, 4) * 8 + lax.rem(i0 + i, 4) * 2 + core
         return pltpu.make_async_remote_copy(
-            src_ref=power.at[pl.ds(t * 8, 8)], dst_ref=rows.at[q], send_sem=ss4.at[core, i], recv_sem=rs4.at[q],
+            src_ref=power.at[pl.ds(t * 8, 8)], dst_ref=rows.at[q], send_sem=ss4, recv_sem=rs4.at[q // (NQ - 1)],
             device_id={"pulse": t}, device_id_type=MESH,
-        )
-
-    def from_bins(s):
-        return pltpu.make_async_remote_copy(
-            src_ref=power.at[pl.ds(s * 8, 8)], dst_ref=rows.at[s], send_sem=ss4.at[0, 0], recv_sem=rs4.at[s],
-            device_id={"pulse": s}, device_id_type=MESH,
         )
 
     for core in range(2):
@@ -355,46 +343,31 @@
         def _():
             to_bins(core, 0).start()
 
-    for part in range(CHUNKS):
-        for h in range(7):
-            hop(h, part)[1].wait_send()
-    for step in range(4):
-        for e in range(2):
-            if GROUPS[step] or e:
-                first_set(step, e).wait_send()
-    for g in range(4):
-        whole = comp.at[g, 1, :, pl.ds(0, 15)]
-        pltpu.make_async_copy(whole, whole, ss2.at[g, 0]).wait()
-    whole = early.at[:, pl.ds(0, 15)]
-    pltpu.make_async_copy(whole, whole, ss6.at[0]).wait()
+    drain(send.at[pl.ds(0, 7)], ss1)
+    drain(early.at[pl.ds(0, NZ - 1)], ss3)
 
     @pl.when(k == 0)
     def _():
-        for g in range(4):
-            whole = comp.at[g, 1, :, 0]
-            pltpu.make_async_copy(whole, whole, ss2.at[g, 1]).wait()
+        drain(comp.at[:, 1], ss2)
+        drain(early.at[:, pl.ds(0, 15)], ss6)
 
     @pl.when(k == 1)
     def _():
-        whole = early.at[:, 0]
-        pltpu.make_async_copy(whole, whole, ss6.at[1]).wait()
-        for step in range(4):
-            for e in range(2):
-                if GROUPS[step] or e:
-                    second_set(step, e).wait_send()
-
-    rows[q] = power[pl.ds(q * 8, 8)]
+        drain(comp.at[:, 1, :, pl.ds(0, 15)], ss2)
+        drain(early, ss6)
+        drain(cols.at[pl.ds(0, NZ - 1)], ss7)
+
+    own_rows = pltpu.make_async_copy(power.at[pl.ds(q * 8, 8)], rows.at[q], stores)
+    own_rows.start()
     outer = NQ - 1
 
-    def store(s):
-        return pltpu.make_async_copy(rows.at[s], rows_hbm.at[s], stores)
-
-    store(q).start()
+    @pl.when(q == outer)
+    def _():
+        own_rows.wait()
 
     @pl.when(q != outer)
     def _():
-        from_bins(outer).wait_recv()
-        store(outer).start()
+        drain(rows.at[outer], rs4.at[1])
 
     edge = pltpu.make_async_remote_copy(
         src_ref=rows.at[outer], dst_ref=halo, send_sem=ss5, recv_sem=rs5,
@@ -402,27 +375,17 @@
     )
     edge.start()
 
-    def wait_bins(d, carry):
-        s = lax.rem(q + d, NQ)
-
-        @pl.when(s != outer)
-        def _():
-            from_bins(s).wait_recv()
-            store(s).start()
-
-        return carry
-
-    lax.fori_loop(1, NQ, wait_bins, 0)
+    @pl.when(q == outer)
+    def _():
+        drain(rows.at[pl.ds(0, NQ - 1)], rs4.at[0])
+
+    @pl.when(q != outer)
+    def _():
+        drain(rows.at[pl.ds(0, NQ - 2)], rs4.at[0])
+        own_rows.wait()
 
     edge.wait()
-    pltpu.make_async_copy(rows, rows_hbm, stores).wait()
-    for core in range(2):
-        for i in NEAR_LAST:
-            to_bins(core, i).wait_send()
-
-        @pl.when(lax.rem(q, 2) == 1 - core)
-        def _():
-            to_bins(core, 0).wait_send()
+    drain(power.at[pl.ds(0, 8 * (NQ - 1))], ss4)
 
 
 def band_table():
@@ -498,15 +461,14 @@
         pltpu.VMEM((8, 32, 16, 128), BF16),
         pltpu.VMEM((256, 16, 128), F32),
         pltpu.VMEM((256, 8, 128), BF16),
-        pltpu.VMEM((32, 8, 8, 128), BF16),
-        dma((4,)), dma((CHUNKS, 4)),
-        dma((7, CHUNKS)), dma((7, CHUNKS)),
-        dma((4, 2)), dma((4,)),
-        dma((4, 2)), dma((4, 2)),
-        dma((2, 16)), dma((32,)),
+        dma((4,)), dma((CHUNKS,)),
+        dma, dma((CHUNKS,)),
+        dma, dma((4,)),
+        dma, dma((4,)),
+        dma, dma((2,)),
         dma, dma,
-        dma((2,)), dma,
-        dma((4, 2)), dma((4, 2)),
+        dma, dma,
+        dma, dma,
         dma,
     ]
     rows, halo = pl.pallas_call(

time: 95.5 us -> 93 us (0.974)
  Pallas kernels: 95.3 us -> 92.9 us
    pallas_call x1, Pallas kernels: 92.8 us -> 90.3 us  [shards(): pl.pallas_call(kernel, out_shape=[jax.ShapeDtypeStruct((32, 8, 8, 128), B...]
where the time goes in v3:
time: 93 us; the launch traced here: 92.9 us
  Pallas kernels  92.9 us (100%)
    pallas_call x1, Pallas kernels, shards(): pl.pallas_call(kernel, out_shape=[jax.ShapeDtypeStruct((32, 8, 8, 128), B...  90.3 us
    pallas_call x1, Pallas kernels, shards(): pl.pallas_call(window, out_shape=jax.ShapeDtypeStruct((64, 4096), F32), i...  2.55 us

profile of v3, /device:TPU:1, one launch (start us, length us, event | category | flops | bytes accessed | tf_op | source)
XLA Modules:
  0.0 92.9 jit_solution(5073688837199312921)
XLA Ops:
  0.0 90.3 %radar.1 = (bf16[32,8,8,128]{3,2,1,0:T(8,128)(2,1)}, bf16[8,8,128]{2,1,0:T(8,128)(2,1)}) custom-call(bf16[2,16,8,4096]{3,2,1,0:T(8,128)(2,1)} %sig_hbm.1, bf16[2,32,64]{2,1,0:T(8,128)(2,1)} %steer_hbm.1, f32[2,8192]{1,0:T(2,128)} %spec_hbm.1, bf16[2,256,256]{2,1,0:T(8,128)(2,1)} %constant.6.clone.lanes_hbm, f32[2,64,128]{2,1,0:T(8,128)} %constant.7.clone.twist_hbm), custom_call_target="tpu_custom_call" | custom-call | tf_op jit(solution)/shard_map/radar/pallas_call | solution.py:474
  90.3 2.5 %window.1 = f32[64,4096]{1,0:T(8,128)} custom-call(bf16[32,8,8,128]{3,2,1,0:T(8,128)(2,1)} %get-tuple-element.7.rows, bf16[8,8,128]{2,1,0:T(8,128)(2,1)} %get-tuple-element.8.halo, bf16[512,256]{1,0:T(8,128)(2,1)} %constant.8.clone.band), custom_call_target="tpu_custom_call" | custom-call | tf_op jit(solution)/shard_map/window/pallas_call | solution.py:483

commit v4 on v3

--- a/solution.py
+++ b/solution.py
@@ -87,11 +87,6 @@
     for d in range(1, NZ):
         pl.semaphore_signal(bar, inc=1, device_id=zdev(lax.rem(me + d, NZ)), device_id_type=MESH)
 
-    def greet(d, carry):
-        pl.semaphore_signal(bar, inc=1, device_id={"pulse": lax.rem(q + d, NQ)}, device_id_type=MESH)
-        return carry
-
-    lax.fori_loop(1, NQ, greet, 0)
     fetched = [
         pltpu.make_async_copy(a, b, loads.at[i])
         for i, (a, b) in enumerate(
@@ -107,7 +102,15 @@
         at = (slice(None), slice(None), slice(None), pl.ds((8 * a + part * per) * 128, per * 128))
         return pltpu.make_async_copy(sig_hbm.at[at], sig.at[at], parts.at[part])
 
-    for part in range(CHUNKS):
+    for a in range(4):
+        part_copy(0, a).start()
+
+    def greet(d, carry):
+        pl.semaphore_signal(bar, inc=1, device_id={"pulse": lax.rem(q + d, NQ)}, device_id_type=MESH)
+        return carry
+
+    lax.fori_loop(1, NQ, greet, 0, unroll=8)
+    for part in range(1, CHUNKS):
         for a in range(4):
             part_copy(part, a).start()
     for copy in fetched:

time: 93 us -> 92.9 us (level)
  no operation moved by 1% of the time
where the time goes in v4:
time: 92.9 us; the launch traced here: 92.8 us
  Pallas kernels  92.8 us (100%)
    pallas_call x1, Pallas kernels, shards(): pl.pallas_call(kernel, out_shape=[jax.ShapeDtypeStruct((32, 8, 8, 128), B...  90.2 us
    pallas_call x1, Pallas kernels, shards(): pl.pallas_call(window, out_shape=jax.ShapeDtypeStruct((64, 4096), F32), i...  2.55 us

profile of v4, /device:TPU:1, one launch (start us, length us, event | category | flops | bytes accessed | tf_op | source)
XLA Modules:
  0.0 92.8 jit_solution(6391190625750225669)
XLA Ops:
  0.0 90.2 %radar.1 = (bf16[32,8,8,128]{3,2,1,0:T(8,128)(2,1)}, bf16[8,8,128]{2,1,0:T(8,128)(2,1)}) custom-call(bf16[2,16,8,4096]{3,2,1,0:T(8,128)(2,1)} %sig_hbm.1, bf16[2,32,64]{2,1,0:T(8,128)(2,1)} %steer_hbm.1, f32[2,8192]{1,0:T(2,128)} %spec_hbm.1, bf16[2,256,256]{2,1,0:T(8,128)(2,1)} %constant.6.clone.lanes_hbm, f32[2,64,128]{2,1,0:T(8,128)} %constant.7.clone.twist_hbm), custom_call_target="tpu_custom_call" | custom-call | tf_op jit(solution)/shard_map/radar/pallas_call | solution.py:477
  90.2 2.5 %window.1 = f32[64,4096]{1,0:T(8,128)} custom-call(bf16[32,8,8,128]{3,2,1,0:T(8,128)(2,1)} %get-tuple-element.7.rows, bf16[8,8,128]{2,1,0:T(8,128)(2,1)} %get-tuple-element.8.halo, bf16[512,256]{1,0:T(8,128)(2,1)} %constant.8.clone.band), custom_call_target="tpu_custom_call" | custom-call | tf_op jit(solution)/shard_map/window/pallas_call | solution.py:486

commit v5 on v4

--- a/solution.py
+++ b/solution.py
@@ -230,11 +230,14 @@
             device_id={"chan": g, "range": rr}, device_id_type=MESH,
         )
 
+    def slot(step):
+        return 2 * ((1 - GROUPS[step]) % 4)
+
     def first_set(step, e):
-        return along(step, e, lambda g, rr: comp.at[g, 0, rr], early.at[me], ss3, rs3.at[step])
+        return along(step, e, lambda g, rr: comp.at[g, 0, rr], early.at[slot(step) + r], ss3, rs3.at[step])
 
     def second_set(step, e):
-        return along(step, e, lambda g, rr: crossed.at[g, rr], cols.at[me], ss7, rs7)
+        return along(step, e, lambda g, rr: crossed.at[g, rr], cols.at[slot(step) + r], ss7, rs7)
 
     def cross(g, i):
         t = chip(i, 1)
@@ -244,11 +247,10 @@
             device_id={"pulse": t}, device_id_type=MESH,
         )
 
-    def forward(cs, i):
+    def forward(at, count, i):
         t = chip(i, 0)
-        pick = pl.ds(2 * cs, 2)
         return pltpu.make_async_remote_copy(
-            src_ref=early.at[pick, t // 2], dst_ref=cols.at[pick, q], send_sem=ss6, recv_sem=rs6,
+            src_ref=early.at[pl.ds(at, count), t // 2], dst_ref=cols.at[pl.ds(at, count), q], send_sem=ss6, recv_sem=rs6,
             device_id={"pulse": t}, device_id_type=MESH,
         )
 
@@ -273,7 +275,7 @@
         filter_group(lax.rem(c + GROUPS[step], 4))
         send_group(step)
     for i in range(16):
-        early[me, i] = comp[c, 0, r, i]
+        early[slot(3) + r, i] = comp[c, 0, r, i]
 
     def second_go(step):
         @pl.when(k == 1)
@@ -284,34 +286,32 @@
                 if GROUPS[step] or e:
                     second_set(step, e).start()
 
-    def first_go(step):
-        cs = lax.rem(c - GROUPS[step] + 4, 4)
-        drain(early.at[pl.ds(0, 2 if GROUPS[step] else 1)], rs3.at[step])
+    def first_go(steps, at, count):
+        for step in steps:
+            drain(early.at[pl.ds(0, 2 if GROUPS[step] else 1)], rs3.at[step])
         for i in NEAR_LAST:
-            forward(cs, i).start()
+            forward(at, count, i).start()
 
         @pl.when(k == 1)
         def _():
-            forward(cs, 0).start()
+            forward(at, count, 0).start()
 
         @pl.when(k == 0)
         def _():
-            for e in range(2):
-                cols[2 * cs + e, q] = early[2 * cs + e, i0]
+            for z in range(at, at + count):
+                cols[z, q] = early[z, i0]
 
     second_go(0)
     second_go(1)
-    first_go(0)
+    first_go((0,), 6, 2)
     second_go(2)
-    first_go(1)
     second_go(3)
-    first_go(2)
-    first_go(3)
+    first_go((1, 2, 3), 0, 6)
 
     @pl.when(k == 1)
     def _():
         def keep(t, carry):
-            cols[me, t] = crossed[c, r, t]
+            cols[slot(3) + r, t] = crossed[c, r, t]
             return carry
 
         lax.fori_loop(0, NQ, keep, 0, unroll=4)
@@ -321,9 +321,10 @@
     def _():
         drain(cols.at[:, pl.ds(0, NQ - 1)], rs6)
 
+    places = [2 * lax.rem(cs - c + 5, 4) for cs in range(4)]
     for b in range(16):
         ps = [16 * a + b for a in range(16)]
-        ys = dft([pair(cols[p % 8, p // 8]) for p in ps], -1)
+        ys = dft([pair(cols[places[p % 8 // 2] + p % 2, p // 8]) for p in ps], -1)
         for fa in range(16):
             dmid[b * 16 + fa] = joined(times(ys[fa], b * fa, 256, -1))
     def to_bins(core, i):
@@ -333,7 +334,7 @@
             device_id={"pulse": t}, device_id_type=MESH,
         )
 
-    for core in range(2):
+    for core in (1, 0):
         for fa in range(core * 8, core * 8 + 8):
             xs = dft([pair(dmid[b * 16 + fa]) for b in range(16)], -1)
             for fb in range(16):

time: 92.9 us -> 91.8 us (0.988)
  Pallas kernels: 92.8 us -> 91.7 us
    pallas_call x1, Pallas kernels: 90.2 us -> 89.1 us  [shards(): pl.pallas_call(kernel, out_shape=[jax.ShapeDtypeStruct((32, 8, 8, 128), B...]
where the time goes in v5:
time: 91.8 us; the launch traced here: 91.7 us
  Pallas kernels  91.7 us (100%)
    pallas_call x1, Pallas kernels, shards(): pl.pallas_call(kernel, out_shape=[jax.ShapeDtypeStruct((32, 8, 8, 128), B...  89.1 us
    pallas_call x1, Pallas kernels, shards(): pl.pallas_call(window, out_shape=jax.ShapeDtypeStruct((64, 4096), F32), i...  2.55 us

profile of v5, /device:TPU:1, one launch (start us, length us, event | category | flops | bytes accessed | tf_op | source)
XLA Modules:
  0.0 91.7 jit_solution(7446167527264521134)
XLA Ops:
  0.0 89.1 %radar.1 = (bf16[32,8,8,128]{3,2,1,0:T(8,128)(2,1)}, bf16[8,8,128]{2,1,0:T(8,128)(2,1)}) custom-call(bf16[2,16,8,4096]{3,2,1,0:T(8,128)(2,1)} %sig_hbm.1, bf16[2,32,64]{2,1,0:T(8,128)(2,1)} %steer_hbm.1, f32[2,8192]{1,0:T(2,128)} %spec_hbm.1, bf16[2,256,256]{2,1,0:T(8,128)(2,1)} %constant.6.clone.lanes_hbm, f32[2,64,128]{2,1,0:T(8,128)} %constant.7.clone.twist_hbm), custom_call_target="tpu_custom_call" | custom-call | tf_op jit(solution)/shard_map/radar/pallas_call | solution.py:478
  89.1 2.6 %window.1 = f32[64,4096]{1,0:T(8,128)} custom-call(bf16[32,8,8,128]{3,2,1,0:T(8,128)(2,1)} %get-tuple-element.7.rows, bf16[8,8,128]{2,1,0:T(8,128)(2,1)} %get-tuple-element.8.halo, bf16[512,256]{1,0:T(8,128)(2,1)} %constant.8.clone.band), custom_call_target="tpu_custom_call" | custom-call | tf_op jit(solution)/shard_map/window/pallas_call | solution.py:487
